TPU v7x, 32 devices: a whole 2x2x4 slice. The times are simulated.
32 devices in a mesh: dp: 16 (over z, x, core), tensor: 2 (over y).
Axes of the slice: x: 2, y: 2, z: 4, core: 2. Of those that a mesh axis runs over, the one named last changes fastest.
Arguments:
- block_input: bfloat16 [32, 577, 1024], P('dp'), may hold values from -6 to 6
- first_scale: float32 [1024], replicated, may hold values from 0.5 to 1.5
- first_shift: float32 [1024], replicated, may hold values from -3 to 3
- heads_weight: bfloat16 [1024, 3, 1024], P(None, None, 'tensor'), may hold values from -0.1875 to 0.1875
- heads_bias: float32 [2, 1024], P(None, 'tensor'), may hold values from -3 to 3
- mixing_weight: bfloat16 [1024, 1024], P('tensor'), may hold values from -0.75 to 0.75
- mixing_bias: float32 [1024], replicated, may hold values from -3 to 3
- second_scale: float32 [1024], replicated, may hold values from 0.5 to 1.5
- second_shift: float32 [1024], replicated, may hold values from -3 to 3
- expand_weight: bfloat16 [1024, 4096], P(None, 'tensor'), may hold values from -0.1875 to 0.1875
- expand_bias: float32 [4096], P('tensor'), may hold values from -3 to 3
- shrink_weight: bfloat16 [4096, 1024], P('tensor'), may hold values from -0.09375 to 0.09375
- shrink_bias: float32 [1024], replicated, may hold values from -3 to 3
- output_grad: bfloat16 [32, 577, 1024], P('dp'), may hold values from -6 to 6
Outputs:
- block_output: bfloat16 [32, 577, 1024], P('dp')
- input_grad: bfloat16 [32, 577, 1024], P('dp')
- heads_weight_grad: float32 [1024, 3, 1024], P(None, None, 'tensor')
- heads_bias_grad: float32 [2, 1024], P(None, 'tensor')
- mixing_weight_grad: float32 [1024, 1024], P('tensor')
- mixing_bias_grad: float32 [1024], replicated
- second_scale_grad: float32 [1024], replicated
- second_shift_grad: float32 [1024], replicated
- expand_weight_grad: float32 [1024, 4096], P(None, 'tensor')
- expand_bias_grad: float32 [4096], P('tensor')
- shrink_weight_grad: float32 [4096, 1024], P('tensor')
- shrink_bias_grad: float32 [1024], replicated
- first_scale_grad: float32 [1024], replicated
- first_shift_grad: float32 [1024], replicated
All inputs are finite; a program needn't handle non-finite values.
Results may differ from a plain program's by a relative error of at most 0.012.
Values sent between devices are 32-bit elements; how exact they have to be, the bound alone decides.
A program may use at most 256 MiB of HBM per device.

v0:
```python
import math
import jax
import jax.numpy as jnp
from jax import lax
from jax.sharding import PartitionSpec as P

HEAD_DIM = 64
EPSILON = 1e-06


def normalize(values):
    center = values - jnp.mean(values, axis=-1, keepdims=True)
    inverse = lax.rsqrt(jnp.mean(center * center, axis=-1, keepdims=True) + EPSILON)
    return (center * inverse, inverse)


def norm_back(grad_out, scale, normed, inverse):
    scaled = grad_out * scale
    return inverse * (
        scaled
        - jnp.mean(scaled, axis=-1, keepdims=True)
        - normed * jnp.mean(scaled * normed, axis=-1, keepdims=True)
    )


def gelu_slope(pre_act):
    cumul = 0.5 * (1.0 + lax.erf(pre_act * 0.7071067811865476))
    return cumul + pre_act * jnp.exp(-0.5 * pre_act * pre_act) * 0.3989422804014327


def cross_dot(left_side, right_side):
    return lax.dot_general(
        left_side, right_side, (((0,), (0,)), ((), ())), preferred_element_type=jnp.float32
    )


def back_dot(left_side, right_side):
    return lax.dot_general(
        left_side, right_side, (((1,), (1,)), ((), ())), preferred_element_type=jnp.float32
    )


def on_device(
    block_input,
    first_scale,
    first_shift,
    heads_weight,
    heads_bias,
    mixing_weight,
    mixing_bias,
    second_scale,
    second_shift,
    expand_weight,
    expand_bias,
    shrink_weight,
    shrink_bias,
    output_grad,
):
    images, length, width = block_input.shape
    local = heads_weight.shape[2]
    heads_here = local // HEAD_DIM
    total_rows = images * length
    factor = 1.0 / math.sqrt(HEAD_DIM)
    head_shape = (images, length, heads_here, HEAD_DIM)
    flat_in = block_input.reshape(total_rows, width).astype(jnp.float32)
    normed_one, inverse_one = normalize(flat_in)
    layer_one = (normed_one * first_scale + first_shift).astype(jnp.bfloat16)
    joined_weight = heads_weight.reshape(width, 3 * local)
    projected = jnp.dot(layer_one, joined_weight, preferred_element_type=jnp.float32).reshape(
        total_rows, 3, local
    )
    queries = (projected[:, 0] + heads_bias[0]).astype(jnp.bfloat16).reshape(head_shape)
    keys_all = projected[:, 1].astype(jnp.bfloat16).reshape(head_shape)
    values_all = (projected[:, 2] + heads_bias[1]).astype(jnp.bfloat16).reshape(head_shape)
    scores = (
        jnp.einsum("bqhd,bkhd->bhqk", queries, keys_all, preferred_element_type=jnp.float32)
        * factor
    )
    logsum = jax.nn.logsumexp(scores, axis=-1, keepdims=True)
    probs_low = jnp.exp(scores - logsum).astype(jnp.bfloat16)
    attended = jnp.einsum(
        "bhqk,bkhd->bqhd", probs_low, values_all, preferred_element_type=jnp.float32
    )
    attended = attended.astype(jnp.bfloat16).reshape(total_rows, local)
    mixed = lax.psum(jnp.dot(attended, mixing_weight, preferred_element_type=jnp.float32), "tensor")
    hidden_one = flat_in + mixed + mixing_bias
    normed_two, inverse_two = normalize(hidden_one)
    layer_two = (normed_two * second_scale + second_shift).astype(jnp.bfloat16)
    pre_act = jnp.dot(layer_two, expand_weight, preferred_element_type=jnp.float32) + expand_bias
    activated = jax.nn.gelu(pre_act, approximate=False).astype(jnp.bfloat16)
    shrunk = lax.psum(
        jnp.dot(activated, shrink_weight, preferred_element_type=jnp.float32), "tensor"
    )
    block_output = (
        (hidden_one + shrunk + shrink_bias).astype(jnp.bfloat16).reshape(images, length, width)
    )
    owner = lax.axis_index("tensor")
    share = images // lax.axis_size("tensor")

    def own_sum(rows_wide):
        picked = lax.dynamic_slice_in_dim(
            rows_wide.reshape(images, length, width), owner * share, share, 0
        )
        return jnp.sum(picked, axis=(0, 1))

    upstream = output_grad.reshape(total_rows, width)
    upstream_wide = upstream.astype(jnp.float32)
    shrink_grad = cross_dot(activated, upstream)
    shrink_bias_part = own_sum(upstream_wide)
    pre_grad = back_dot(upstream, shrink_weight) * gelu_slope(pre_act)
    pre_low = pre_grad.astype(jnp.bfloat16)
    expand_bias_grad = jnp.sum(pre_grad, axis=0)
    expand_grad = cross_dot(layer_two, pre_low)
    partial_two = back_dot(pre_low, expand_weight)
    second_scale_part = jnp.sum(partial_two * normed_two, axis=0)
    second_shift_part = jnp.sum(partial_two, axis=0)
    layer_two_grad = lax.psum(partial_two, "tensor")
    hidden_grad = upstream_wide + norm_back(layer_two_grad, second_scale, normed_two, inverse_two)
    mixing_bias_part = own_sum(hidden_grad)
    hidden_low = hidden_grad.astype(jnp.bfloat16)
    mixing_grad = cross_dot(attended, hidden_low)
    attended_grad = back_dot(hidden_low, mixing_weight).astype(jnp.bfloat16).reshape(head_shape)
    scores = (
        jnp.einsum("bqhd,bkhd->bhqk", queries, keys_all, preferred_element_type=jnp.float32)
        * factor
    )
    probs = jnp.exp(scores - logsum)
    values_grad = jnp.einsum(
        "bhqk,bqhd->bkhd",
        probs.astype(jnp.bfloat16),
        attended_grad,
        preferred_element_type=jnp.float32,
    )
    probs_grad = jnp.einsum(
        "bqhd,bkhd->bhqk", attended_grad, values_all, preferred_element_type=jnp.float32
    )
    row_dot = jnp.sum(probs * probs_grad, axis=-1, keepdims=True)
    score_low = (probs * (probs_grad - row_dot) * factor).astype(jnp.bfloat16)
    queries_grad = jnp.einsum(
        "bhqk,bkhd->bqhd", score_low, keys_all, preferred_element_type=jnp.float32
    )
    keys_grad = jnp.einsum(
        "bhqk,bqhd->bkhd", score_low, queries, preferred_element_type=jnp.float32
    )
    stacked = jnp.stack(
        [
            queries_grad.reshape(total_rows, local),
            keys_grad.reshape(total_rows, local),
            values_grad.reshape(total_rows, local),
        ],
        axis=1,
    )
    heads_bias_grad = jnp.stack([jnp.sum(stacked[:, 0], axis=0), jnp.sum(stacked[:, 2], axis=0)])
    stacked_low = stacked.astype(jnp.bfloat16).reshape(total_rows, 3 * local)
    heads_grad = cross_dot(layer_one, stacked_low).reshape(width, 3, local)
    partial_one = back_dot(stacked_low, joined_weight)
    first_scale_part = jnp.sum(partial_one * normed_one, axis=0)
    first_shift_part = jnp.sum(partial_one, axis=0)
    layer_one_grad = lax.psum(partial_one, "tensor")
    input_grad = hidden_grad + norm_back(layer_one_grad, first_scale, normed_one, inverse_one)
    input_grad = input_grad.astype(jnp.bfloat16).reshape(images, length, width)
    bias_heads_sum, bias_expand_sum = lax.psum((heads_bias_grad, expand_bias_grad), "dp")
    (
        first_scale_sum,
        first_shift_sum,
        second_scale_sum,
        second_shift_sum,
        mixing_bias_sum,
        shrink_bias_sum,
    ) = lax.psum(
        (
            first_scale_part,
            first_shift_part,
            second_scale_part,
            second_shift_part,
            mixing_bias_part,
            shrink_bias_part,
        ),
        ("dp", "tensor"),
    )
    weight_part = (
        lax.psum_scatter(heads_grad, "dp", scatter_dimension=0, tiled=True),
        lax.psum_scatter(mixing_grad, "dp", scatter_dimension=0, tiled=True),
        lax.psum_scatter(expand_grad, "dp", scatter_dimension=0, tiled=True),
        lax.psum_scatter(shrink_grad, "dp", scatter_dimension=0, tiled=True),
    )
    heads_full, mixing_full, expand_full, shrink_full = (
        lax.all_gather(weight_part[0], "dp", axis=0, tiled=True),
        lax.all_gather(weight_part[1], "dp", axis=0, tiled=True),
        lax.all_gather(weight_part[2], "dp", axis=0, tiled=True),
        lax.all_gather(weight_part[3], "dp", axis=0, tiled=True),
    )
    return (
        block_output,
        input_grad,
        heads_full,
        bias_heads_sum,
        mixing_full,
        mixing_bias_sum,
        second_scale_sum,
        second_shift_sum,
        expand_full,
        bias_expand_sum,
        shrink_full,
        shrink_bias_sum,
        first_scale_sum,
        first_shift_sum,
    )


def solution(mesh):
    placed = (
        P("dp", None, None),
        P(),
        P(),
        P(None, None, "tensor"),
        P(None, "tensor"),
        P("tensor", None),
        P(),
        P(),
        P(),
        P(None, "tensor"),
        P("tensor"),
        P("tensor", None),
        P(),
        P("dp", None, None),
    )
    return jax.shard_map(
        on_device,
        mesh=mesh,
        in_specs=placed,
        out_specs=(
            P("dp", None, None),
            P("dp", None, None),
            P(None, None, "tensor"),
            P(None, "tensor"),
            P("tensor", None),
            P(),
            P(),
            P(),
            P(None, "tensor"),
            P("tensor"),
            P("tensor", None),
            P(),
            P(),
            P(),
        ),
        check_vma=False,
    )
```

profile of v0, /device:TPU:0, one launch (start us, length us, event | category | flops | bytes accessed | tf_op | source)
XLA Modules:
  0.0 1360.8 jit_solution(9283532576933548809)
XLA Ops:
  7.3 3.7 convert_reduce_fusion
  11.1 3.2 multiply_reduce_fusion.7
  15.1 4.7 add_convert_fusion.3
  22.0 3.6 reshape.213
  25.5 4.6 copy.114
  30.2 6.5 fusion.29
  36.7 2.7 fusion.64
  40.6 4.6 reshape.217
  45.1 5.1 copy.118
  50.2 4.1 reshape.221
  54.3 4.2 copy.120
  58.6 14.0 %multiply_reduce_fusion.1 = (f32[2,8,577]{2,1,0:T(8,128)S(1)}, f32[2,8,577,577]{2,3,1,0:T(8,128)}) fusion(bf16[2,577,8,64]{1,3,2,0:T(8,128)(2,1)} %copy.120, f32[2,577,8,64]{1,3,2,0:T(8,128)} %copy.118, f32[8,64]{1,0:T(8,128)S(1)} %add.150), kind=kOutput, calls=%fused_computation.6 | convolution fusion | flops 693664768 | bytes 24891520 | tf_op jit(solution)/shard_map/bqhd,bkhd->bhqk/dot_general | solution.py:76
  72.6 10.4 exponential_reduce_fusion
  83.0 4.6 reshape.216
  87.6 5.0 copy.116
  94.7 12.8 fusion.48
  109.9 4.4 reshape.206
  114.3 4.9 fusion.70
  119.3 3.1 copy.108
  122.4 5.0 reshape.212
  127.4 2.7 copy.123
  132.0 110.1 %all-reduce.7.cloned.1.call-done = f32[1154,1024]{1,0:T(8,128)} async-done(((f32[1154,1024]{1,0:T(8,128)}), f32[1154,1024]{1,0:T(8,128)}) %all-reduce.7.cloned.1.call-update) | async-done | bytes 4726800 | tf_op jit(solution)/shard_map/psum | solution.py:85
  242.1 4.4 fusion.63
  247.2 3.2 copy-done.42
  250.5 28.3 %fusion.7 = (bf16[1154,2048]{1,0:T(8,128)(2,1)}, f32[1154,2048]{1,0:T(8,128)}) fusion(f32[2048]{0:T(1024)S(1)} %copy-done.44, bf16[1024,2048]{1,0:T(8,128)(2,1)S(1)} %copy-done.42, f32[1154,1024]{1,0:T(8,128)S(1)} %get-tuple-element.91, f32[1024]{0:T(1024)S(1)} %copy-done.45, f32[1024]{0:T(1024)S(1)} %copy-done.35, f32[1154]{0:T(1024)S(1)} %add_rsqrt_fusion.1, ...), kind=kOutput, calls=%fused_computation.14 | convolution fusion | flops 5002119168 | bytes 23127056 | tf_op jit(solution)/shard_map/dot_general | solution.py:89
  278.7 10.9 fusion.69
  291.9 6.8 fusion.33
  298.7 120.1 %all-reduce.9.cloned.1.call-done = f32[1154,1024]{1,0:T(8,128)} async-done(((f32[1154,1024]{1,0:T(8,128)}), f32[1154,1024]{1,0:T(8,128)}) %all-reduce.9.cloned.1.call-update) | async-done | bytes 4726800 | tf_op jit(solution)/shard_map/psum | solution.py:117
  418.8 7.2 multiply_reduce_fusion.3
  426.0 3.4 multiply_add_fusion
  431.7 2.9 fusion.51
  437.2 4.1 copy.125
  441.3 13.8 %fusion.72 = f32[2,8,577,577]{2,3,1,0:T(8,128)} fusion(bf16[2,577,8,64]{1,3,2,0:T(8,128)(2,1)} %copy.125, bf16[2,577,8,64]{1,3,2,0:T(8,128)(2,1)S(1)} %copy-done.8), kind=kOutput, calls=%fused_computation.107 | convolution fusion | flops 681838592 | bytes 23670848 | tf_op jit(solution)/shard_map/bqhd,bkhd->bhqk/dot_general | solution.py:134
  455.2 27.6 %fusion.66 = (f32[8,64]{1,0:T(8,128)S(1)}, bf16[2,577,8,64]{1,3,2,0:T(8,128)(2,1)}) fusion(bf16[2,577,8,64]{1,3,2,0:T(8,128)(2,1)} %copy.120, f32[2,8,577,577]{2,3,1,0:T(8,128)} %fusion.72, f32[2,8,577]{2,1,0:T(8,128)S(1)} %copy-done.26, f32[2,8,577,577]{2,3,1,0:T(8,128)} %get-tuple-element.95, bf16[2,577,8,64]{1,3,2,0:T(8,128)(2,1)} %copy.125, ...), kind=kOutput, calls=%fused_computation.103 | convolution fusion | flops 1412809728 | bytes 47380672 | tf_op jit(solution)/shard_map/bhqk,bkhd->bqhd/dot_general | solution.py:139
  482.8 3.9 copy.150
  486.8 4.2 reshape.218
  491.0 27.1 %fusion.39 = bf16[2,577,8,64]{1,3,2,0:T(8,128)(2,1)} fusion(f32[2,8,577,577]{2,3,1,0:T(8,128)} %fusion.72, f32[2,8,577]{2,1,0:T(8,128)S(1)} %copy-done.26, f32[2,8,577,577]{2,3,1,0:T(8,128)} %get-tuple-element.95, bf16[2,577,8,64]{1,3,2,0:T(8,128)(2,1)} %copy.125, bf16[2,577,8,64]{1,3,2,0:T(8,128)(2,1)S(1)} %copy-done.8, f32[2,577,8,64]{1,3,2,0:T(8,128)} %copy.118, ...), kind=kOutput, calls=%fused_computation.72 | convolution fusion | flops 1412810240 | bytes 48562368 | tf_op jit(solution)/shard_map/bhqk,bqhd->bkhd/dot_general | solution.py:142
  518.1 4.0 copy.151
  522.1 4.2 reshape.219
  526.3 11.1 fusion.65
  537.5 3.7 copy.152
  543.9 9.7 fusion.27
  554.3 11.4 fusion.31
  567.6 10.6 fusion.73
  579.1 10.1 fusion.71
  589.2 5.7 convolution_bitcast_fusion
  594.9 44.0 %reduce-scatter.5.cloned.1.call-done = f32[64,3,512]{2,0,1:T(8,128)} async-done(((f32[1024,3,512]{2,0,1:T(8,128)}), f32[64,3,512]{2,0,1:T(8,128)}) %reduce-scatter.5.cloned.1.call-update) | async-done | bytes 393232 | tf_op jit(solution)/shard_map/reduce_scatter | solution.py:182
  639.0 107.1 %reduce-scatter.9.cloned.1.call-done = f32[64,2048]{1,0:T(8,128)} async-done(((f32[1024,2048]{1,0:T(8,128)}), f32[64,2048]{1,0:T(8,128)}) %reduce-scatter.9.cloned.1.call-update) | async-done | bytes 524304 | tf_op jit(solution)/shard_map/reduce_scatter | solution.py:184
  746.1 107.5 %reduce-scatter.11.cloned.1.call-done = f32[128,1024]{1,0:T(8,128)} async-done(((f32[2048,1024]{1,0:T(8,128)}), f32[128,1024]{1,0:T(8,128)}) %reduce-scatter.11.cloned.1.call-update) | async-done | bytes 524304 | tf_op jit(solution)/shard_map/reduce_scatter | solution.py:185
  854.2 3.1 fusion.35
  857.3 5.1 reshape.211
  862.6 60.9 %all-reduce.1 = (f32[2,512]{1,0:T(2,128)}, f32[2048]{0:T(1024)}) all-reduce(f32[2,512]{1,0:T(2,128)S(1)} %pad_maximum_fusion, f32[2048]{0:T(1024)S(1)} %copy-done.37), channel_id=1, replica_groups=mesh['dp'=16,'tensor'=2] {'dp'}, use_global_device_ids=true, to_apply=%region_18.0 | all-reduce | flops 3072 | bytes 24576 | tf_op jit(solution)/shard_map/psum | solution.py:162
  925.5 195.1 %all-reduce.11.cloned.1.call-done = (f32[1154,1024]{1,0:T(8,128)}, f32[1154,1024]{1,0:T(8,128)}) async-done(((f32[1154,1024]{1,0:T(8,128)}, f32[1154,1024]{1,0:T(8,128)}), (f32[1154,1024]{1,0:T(8,128)}, f32[1154,1024]{1,0:T(8,128)})) %all-reduce.11.cloned.1.call-update) | async-done | bytes 9453584 | tf_op jit(solution)/shard_map/psum | solution.py:91
  1120.6 6.4 multiply_reduce_fusion.2
  1128.4 4.4 add_convert_fusion
  1134.9 3.8 copy.140
  1138.8 5.0 add_convert_fusion.1
  1146.0 3.8 copy.139
  1149.8 42.4 %all-reduce = (f32[1024]{0:T(1024)}, f32[1024]{0:T(1024)}, f32[1024]{0:T(1024)}, f32[1024]{0:T(1024)}, f32[1024]{0:T(1024)}, /*index=5*/f32[1024]{0:T(1024)}) all-reduce(f32[1024]{0:T(1024)S(1)} %dynamic-slice_reduce_fusion, f32[1024]{0:T(1024)S(1)} %copy-done.33, ...), channel_id=1, replica_groups=mesh['dp'=16,'tensor'=2] {'dp','tensor'}, use_global_device_ids=true, to_apply=%region_21.0 | all-reduce | flops 6144 | bytes 49152 | tf_op jit(solution)/shard_map/psum | solution.py:170
  1192.2 69.0 %all-gather.9.cloned.1.call-done = f32[1024,2048]{1,0:T(8,128)} async-done(((f32[64,2048]{1,0:T(8,128)}), f32[1024,2048]{1,0:T(8,128)}) %all-gather.9.cloned.1.call-update) | async-done | bytes 8388624 | tf_op jit(solution)/shard_map/all_gather | solution.py:190
  1261.2 75.1 %all-gather.11.cloned.1.call-done = f32[2048,1024]{1,0:T(8,128)} async-done(((f32[128,1024]{1,0:T(8,128)}), f32[2048,1024]{1,0:T(8,128)}) %all-gather.11.cloned.1.call-update) | async-done | bytes 8388624 | tf_op jit(solution)/shard_map/all_gather | solution.py:191
  1336.3 6.9 copy.172
  1344.9 4.3 copy.174
  1350.7 3.4 copy.175
  (162 shorter events, 36.3 us)
Async XLA Ops:
  7.2 107.1 %copy-start = (bf16[512,1024]{1,0:T(8,128)(2,1)S(1)}, bf16[512,1024]{1,0:T(8,128)(2,1)}, u32[]{:S(2)}) copy-start(bf16[512,1024]{1,0:T(8,128)(2,1)} %param.19) | copy-start | bytes 3145732
  7.2 3.8 copy-start.4
  7.2 7.9 copy-start.31
  7.2 7.9 copy-start.41
  7.2 234.9 %all-reduce.7.cloned.1.call-start = ((), (), s32[]{:S(2)}) async-start(), calls=%async_computation.4 | async-start | bytes 9502720 | tf_op jit(solution)/shard_map/psum | solution.py:85
  11.0 3.3 copy-start.15
  14.4 0.8 copy-start.19
  50.2 8.3 copy-start.40
  58.6 14.0 %copy-start.29 = (f32[8,64]{1,0:T(8,128)}, f32[8,64]{1,0:T(8,128)S(1)}, u32[]{:S(2)}) copy-start(f32[8,64]{1,0:T(8,128)S(1)} %add.150) | copy-start | bytes 6148
  83.0 11.6 copy-start.25
  94.7 12.8 copy-start.7
  119.3 299.5 %all-reduce.9.cloned.1.call-start = ((), (), s32[]{:S(2)}) async-start(), calls=%async_computation.5 | async-start | bytes 9502720 | tf_op jit(solution)/shard_map/psum | solution.py:117
  127.4 114.8 %copy-start.38 = (f32[1024]{0:T(1024)S(1)}, f32[1024]{0:T(1024)}, u32[]{:S(2)}) copy-start(f32[1024]{0:T(1024)} %param.20) | copy-start | bytes 12292
  246.5 32.2 %copy-start.2 = (f32[1154,1024]{1,0:T(8,128)}, f32[1154,1024]{1,0:T(8,128)S(1)}, u32[]{:S(2)}) copy-start(f32[1154,1024]{1,0:T(8,128)S(1)} %get-tuple-element.91) | copy-start | bytes 14180356
  246.5 0.7 copy-start.35
  246.5 3.9 copy-start.42
  246.5 3.9 copy-start.44
  246.5 3.9 copy-start.45
  250.4 175.5 %copy-start.27 = (f32[1154]{0:T(1024)}, f32[1154]{0:T(1024)S(1)}, u32[]{:S(2)}) copy-start(f32[1154]{0:T(1024)S(1)} %add_rsqrt_fusion.1) | copy-start | bytes 13852
  250.4 28.3 %copy-start.10 = (bf16[1154,1024]{1,0:T(8,128)(2,1)S(1)}, bf16[1154,1024]{1,0:T(8,128)(2,1)}, u32[]{:S(2)}) copy-start(bf16[1154,1024]{1,0:T(8,128)(2,1)} %reshape.208) | copy-start | bytes 7090180
  250.4 28.3 %copy-start.43 = (bf16[2048,1024]{1,0:T(8,128)(2,1)S(1)}, bf16[2048,1024]{1,0:T(8,128)(2,1)}, u32[]{:S(2)}) copy-start(bf16[2048,1024]{1,0:T(8,128)(2,1)} %param.25) | copy-start | bytes 12582916
  289.7 2.2 copy-start.47
  298.7 279.7 %reduce-scatter.7.cloned.1.call-start = ((), (), s32[]{:S(2)}) async-start(), calls=%async_computation.8 | async-start | bytes 2228224 | tf_op jit(solution)/shard_map/reduce_scatter | solution.py:183
  418.8 7.2 copy-start.6
  429.4 2.2 copy-start.3
  429.4 2.3 copy-start.14
  434.6 6.8 copy-start.8
  441.3 13.9 %copy-start.26 = (f32[2,8,577]{2,1,0:T(8,128)S(1)}, f32[2,8,577]{2,1,0:T(8,128)}, u32[]{:S(2)}) copy-start(f32[2,8,577]{2,1,0:T(8,128)} %copy-done.25) | copy-start | bytes 110788
  441.3 197.6 %reduce-scatter.5.cloned.1.call-start = ((), (), s32[]{:S(2)}) async-start(), calls=%async_computation.6 | async-start | bytes 6684672 | tf_op jit(solution)/shard_map/reduce_scatter | solution.py:182
  482.8 8.2 copy-start.30
  518.1 8.3 copy-start.9
  553.6 0.7 copy-start.28
  553.6 0.7 copy-start.36
  553.6 0.7 copy-start.46
  553.6 192.4 %reduce-scatter.9.cloned.1.call-start = ((), (), s32[]{:S(2)}) async-start(), calls=%async_computation.10 | async-start | bytes 8912896 | tf_op jit(solution)/shard_map/reduce_scatter | solution.py:184
  565.7 1.9 copy-start.11
  565.8 287.9 %reduce-scatter.11.cloned.1.call-start = ((), (), s32[]{:S(2)}) async-start(), calls=%async_computation.12 | async-start | bytes 8912896 | tf_op jit(solution)/shard_map/reduce_scatter | solution.py:185
  578.3 347.2 %all-gather.7.cloned.1.call-start = ((), (), s32[]{:S(2)}) async-start(), calls=%async_computation.9 | async-start | bytes 2228224 | tf_op jit(solution)/shard_map/all_gather | solution.py:189
  579.0 10.2 copy-start.22
  579.0 10.2 copy-start.23
  579.0 541.6 %all-reduce.11.cloned.1.call-start = ((), (), s32[]{:S(2)}) async-start(), calls=%async_computation.14 | async-start | bytes 19005440 | tf_op jit(solution)/shard_map/psum | solution.py:91
  579.1 10.1 copy-start.18
  579.1 10.1 copy-start.24
  594.9 258.8 %copy-start.20 = (f32[2,577]{0,1:T(8,128)S(1)}, f32[2,577]{0,1:T(8,128)}, u32[]{:S(2)}) copy-start(f32[2,577]{0,1:T(8,128)} %copy-done.19) | copy-start | bytes 13852
  594.9 259.0 %copy-start.16 = (f32[2,577]{0,1:T(8,128)S(1)}, f32[2,577]{0,1:T(8,128)}, u32[]{:S(2)}) copy-start(f32[2,577]{0,1:T(8,128)} %copy-done.15) | copy-start | bytes 13852
  594.9 259.3 %copy-start.12 = (bf16[2,577,1024]{2,0,1:T(2,128)(2,1)S(1)}, bf16[2,577,1024]{2,0,1:T(2,128)(2,1)}, u32[]{:S(2)}) copy-start(bf16[2,577,1024]{2,0,1:T(2,128)(2,1)} %param.27) | copy-start | bytes 7090180
  594.9 597.3 %all-gather.5.cloned.1.call-start = ((), (), s32[]{:S(2)}) async-start(), calls=%async_computation.7 | async-start | bytes 6684672 | tf_op jit(solution)/shard_map/all_gather | solution.py:188
  639.0 622.2 %all-gather.9.cloned.1.call-start = ((), (), s32[]{:S(2)}) async-start(), calls=%async_computation.11 | async-start | bytes 8912896 | tf_op jit(solution)/shard_map/all_gather | solution.py:190
  746.1 590.2 %all-gather.11.cloned.1.call-start = ((), (), s32[]{:S(2)}) async-start(), calls=%async_computation.13 | async-start | bytes 8912896 | tf_op jit(solution)/shard_map/all_gather | solution.py:191
  857.3 5.3 copy-start.37
  857.3 263.3 %copy-start.32 = (f32[1024]{0:T(1024)S(1)}, f32[1024]{0:T(1024)}, u32[]{:S(2)}) copy-start(f32[1024]{0:T(1024)} %param.15) | copy-start | bytes 12292
  857.3 269.8 %slice-start = ((s8[4751360]{0:T(1024)(128)(4,1)}), s8[557056]{0:T(1024)(128)(4,1)S(1)}, s32[]{:S(2)}) async-start(s8[4751360]{0:T(1024)(128)(4,1)} %bitcast.64), calls=%async_computation.15 | async-start | bytes 1114112
  1120.6 6.5 slice-start.1
  1120.6 7.8 copy-start.5
  1132.7 6.0 copy-start.39
  1134.9 3.9 copy-start.17
  1143.8 6.0 copy-start.33
  1143.8 6.0 copy-start.34
  1336.3 6.9 copy-start.21
  1336.3 8.6 copy-start.13
  1343.2 5.9 slice-start.2
  1344.9 5.8 slice-start.3
  1344.9 9.2 copy-start.1
Sparse Core Ops, SparseCore 0:
  119.4 122.6 all-reduce.6
  298.8 119.9 all-reduce.8
  441.4 61.8 reduce-scatter.6
  553.7 85.1 reduce-scatter.4
  643.4 102.5 reduce-scatter.8
  750.6 103.0 reduce-scatter.10
  855.8 41.3 all-gather.6
  899.8 220.8 all-reduce.10
  1122.8 63.2 all-gather.4
  1188.1 73.0 all-gather.8
  1263.4 72.8 all-gather.10
where the time goes:
time: 1370 us; the launch traced here: 1360 us
  waiting for transfers between devices  829 us (61%)
  matrix products  216 us (16%)
  local copies, waits for them, and re-layouts  137 us (10%)
  blocking collectives  103 us (8%)
  other arithmetic  60.6 us (4%)
  between operations  14.6 us (1%)
    psum x1, waiting for transfers between devices, on_device(): lax.psum(jnp.dot(activated, shrink_weight, preferred_element_type=jnp.flo...  195 us
    psum x1, waiting for transfers between devices, on_device(): layer_two_grad = lax.psum(partial_two, 'tensor')  120 us
    psum x1, waiting for transfers between devices, on_device(): lax.psum(jnp.dot(attended, mixing_weight, preferred_element_type=jnp.floa...  110 us
    reduce_scatter x1, waiting for transfers between devices, on_device(): lax.psum_scatter(shrink_grad, 'dp', scatter_dimension=0, tiled=True)  108 us
    reduce_scatter x1, waiting for transfers between devices, on_device(): lax.psum_scatter(expand_grad, 'dp', scatter_dimension=0, tiled=True)  107 us
    all_gather x1, waiting for transfers between devices, on_device(): lax.all_gather(weight_part[3], 'dp', axis=0, tiled=True)  75.1 us
    all_gather x1, waiting for transfers between devices, on_device(): lax.all_gather(weight_part[2], 'dp', axis=0, tiled=True)  69 us
    psum x1, blocking collectives, on_device(): lax.psum((heads_bias_grad, expand_bias_grad), 'dp')  60.9 us
  transfers between devices with their start and end apart: 11, of which 8 were waited for; matrix products, arithmetic and copies ran while one was open for 15% of the time, Pallas kernels for 0%

commit v1 on v0

--- a/solution.py
+++ b/solution.py
@@ -114,7 +114,8 @@
     partial_two = back_dot(pre_low, expand_weight)
     second_scale_part = jnp.sum(partial_two * normed_two, axis=0)
     second_shift_part = jnp.sum(partial_two, axis=0)
-    layer_two_grad = lax.psum(partial_two, "tensor")
+    shards = lax.all_gather(partial_two, "tensor")
+    layer_two_grad = jnp.sum(shards, axis=0)
     hidden_grad = upstream_wide + norm_back(layer_two_grad, second_scale, normed_two, inverse_two)
     mixing_bias_part = own_sum(hidden_grad)
     hidden_low = hidden_grad.astype(jnp.bfloat16)

time: 1370 us -> 1310 us (0.956)
  waiting for transfers between devices: 829 us -> 767 us
    psum x1 -> x0, waiting for transfers between devices: 120 us -> none  [on_device(): layer_two_grad = lax.psum(partial_two, 'tensor')]
    all_gather x0 -> x1, waiting for transfers between devices: none -> 119 us  [on_device(): shards = lax.all_gather(partial_two, 'tensor')]
    reduce_scatter x1, waiting for transfers between devices: 107 us -> 4.49 us  [on_device(): lax.psum_scatter(expand_grad, 'dp', scatter_dimension=0, tiled=True)]
    all_gather x1, waiting for transfers between devices: 69 us -> 4.84 us  [on_device(): lax.all_gather(weight_part[2], 'dp', axis=0, tiled=True)]
    all_gather x1, waiting for transfers between devices: 0.01 us -> 62.3 us  [on_device(): lax.all_gather(weight_part[0], 'dp', axis=0, tiled=True)]
    reduce_scatter x1, waiting for transfers between devices: 44 us -> 89 us  [on_device(): lax.psum_scatter(heads_grad, 'dp', scatter_dimension=0, tiled=True)]
    unnamed x114 -> x102, local copies, waits for them, and re-layouts: 44 us -> 46 us
  transfers between devices with their start and end apart: 11 -> 11, of which waited for: 8 -> 9; matrix products, arithmetic and copies ran while one was open for 15% -> 16% of each run, Pallas kernels for 0% -> 0%
where the time goes in v1:
time: 1310 us
  waiting for transfers between devices  767 us (59%)
  matrix products  218 us (17%)
  local copies, waits for them, and re-layouts  140 us (11%)
  blocking collectives  103 us (8%)
  other arithmetic  65.9 us (5%)
  between operations  14.6 us (1%)
    psum x1, waiting for transfers between devices, on_device(): lax.psum(jnp.dot(activated, shrink_weight, preferred_element_type=jnp.flo...  194 us
    all_gather x1, waiting for transfers between devices, on_device(): shards = lax.all_gather(partial_two, 'tensor')  119 us
    psum x1, waiting for transfers between devices, on_device(): lax.psum(jnp.dot(attended, mixing_weight, preferred_element_type=jnp.floa...  110 us
    reduce_scatter x1, waiting for transfers between devices, on_device(): lax.psum_scatter(shrink_grad, 'dp', scatter_dimension=0, tiled=True)  108 us
    reduce_scatter x1, waiting for transfers between devices, on_device(): lax.psum_scatter(heads_grad, 'dp', scatter_dimension=0, tiled=True)  89 us
    all_gather x1, waiting for transfers between devices, on_device(): lax.all_gather(weight_part[3], 'dp', axis=0, tiled=True)  75.1 us
    all_gather x1, waiting for transfers between devices, on_device(): lax.all_gather(weight_part[0], 'dp', axis=0, tiled=True)  62.3 us
    psum x1, blocking collectives, on_device(): lax.psum((heads_bias_grad, expand_bias_grad), 'dp')  59.3 us
  transfers between devices with their start and end apart: 11, of which 9 were waited for; matrix products, arithmetic and copies ran while one was open for 16% of the time, Pallas kernels for 0%

profile of v1, /device:TPU:0, one launch (start us, length us, event | category | flops | bytes accessed | tf_op | source)
XLA Modules:
  0.0 1308.8 jit_solution(16055191922737678301)
XLA Ops:
  7.3 3.7 convert_reduce_fusion
  11.1 3.2 multiply_reduce_fusion.7
  15.1 4.7 add_convert_fusion.3
  21.9 3.6 reshape.217
  25.5 4.6 copy.114
  30.1 6.5 fusion.29
  40.5 4.6 reshape.221
  45.1 5.0 copy.118
  50.1 4.1 reshape.225
  54.2 4.2 copy.120
  58.5 14.0 %multiply_reduce_fusion.1 = (f32[2,8,577]{2,1,0:T(8,128)S(1)}, f32[2,8,577,577]{2,3,1,0:T(8,128)}) fusion(bf16[2,577,8,64]{1,3,2,0:T(8,128)(2,1)} %copy.120, f32[2,577,8,64]{1,3,2,0:T(8,128)} %copy.118, f32[8,64]{1,0:T(8,128)S(1)} %add.148), kind=kOutput, calls=%fused_computation.6 | convolution fusion | flops 693664768 | bytes 24891520 | tf_op jit(solution)/shard_map/bqhd,bkhd->bhqk/dot_general | solution.py:76
  72.5 10.4 exponential_reduce_fusion
  83.0 4.6 reshape.220
  87.6 5.0 copy.116
  94.6 12.8 fusion.48
  109.9 4.4 reshape.206
  114.3 4.9 fusion.70
  119.3 3.1 copy.108
  122.3 5.0 reshape.212
  131.9 110.1 %all-reduce.6.cloned.1.call-done = f32[1154,1024]{1,0:T(8,128)} async-done(((f32[1154,1024]{1,0:T(8,128)}), f32[1154,1024]{1,0:T(8,128)}) %all-reduce.6.cloned.1.call-update) | async-done | bytes 4726800 | tf_op jit(solution)/shard_map/psum | solution.py:85
  242.1 4.4 fusion.63
  247.2 3.2 copy-done.35
  250.4 28.1 %fusion.7 = (bf16[1154,2048]{1,0:T(8,128)(2,1)}, f32[1154,2048]{1,0:T(8,128)}) fusion(f32[2048]{0:T(1024)S(1)} %copy-done.37, bf16[1024,2048]{1,0:T(8,128)(2,1)S(1)} %copy-done.35, f32[1154,1024]{1,0:T(8,128)S(1)} %get-tuple-element.91, f32[1024]{0:T(1024)S(1)} %copy-done.38, f32[1024]{0:T(1024)S(1)} %copy-done.29, f32[1154]{0:T(1024)S(1)} %add_rsqrt_fusion.1, ...), kind=kOutput, calls=%fused_computation.14 | convolution fusion | flops 5002119168 | bytes 23127056 | tf_op jit(solution)/shard_map/dot_general | solution.py:89
  278.5 10.9 fusion.69
  289.4 6.8 fusion.33
  296.3 118.8 %all-gather.16.cloned.1.call-done = f32[2,1154,1024]{2,1,0:T(8,128)} async-done(((f32[1,1154,1024]{2,1,0:T(8,128)}), f32[2,1154,1024]{2,1,0:T(8,128)}) %all-gather.16.cloned.1.call-update) | async-done | bytes 9453584 | tf_op jit(solution)/shard_map/all_gather | solution.py:117
  415.1 7.4 reduce_sum.185
  422.5 6.6 multiply_reduce_fusion.3
  434.9 2.8 fusion.51
  437.8 11.4 fusion.31
  451.0 10.4 fusion.73
  461.5 3.8 convolution_convert_fusion
  467.9 4.3 copy.125
  472.2 13.3 %fusion.72 = f32[2,8,577,577]{2,3,1,0:T(8,128)} fusion(bf16[2,577,8,64]{1,3,2,0:T(8,128)(2,1)} %copy.125, bf16[2,577,8,64]{1,3,2,0:T(8,128)(2,1)S(1)} %copy-done.7), kind=kOutput, calls=%fused_computation.107 | convolution fusion | flops 681838592 | bytes 23670848 | tf_op jit(solution)/shard_map/bqhd,bkhd->bhqk/dot_general | solution.py:135
  485.5 26.9 %fusion.66 = (f32[8,64]{1,0:T(8,128)S(1)}, bf16[2,577,8,64]{1,3,2,0:T(8,128)(2,1)}) fusion(bf16[2,577,8,64]{1,3,2,0:T(8,128)(2,1)} %copy.120, f32[2,8,577,577]{2,3,1,0:T(8,128)} %fusion.72, f32[2,8,577]{2,1,0:T(8,128)S(1)} %copy-done.24, f32[2,8,577,577]{2,3,1,0:T(8,128)} %get-tuple-element.95, bf16[2,577,8,64]{1,3,2,0:T(8,128)(2,1)} %copy.125, ...), kind=kOutput, calls=%fused_computation.103 | convolution fusion | flops 1412809728 | bytes 47380672 | tf_op jit(solution)/shard_map/bhqk,bkhd->bqhd/dot_general | solution.py:140
  512.4 4.1 copy.150
  516.5 4.4 reshape.222
  520.9 28.8 %fusion.39 = bf16[2,577,8,64]{1,3,2,0:T(8,128)(2,1)} fusion(f32[2,8,577,577]{2,3,1,0:T(8,128)} %fusion.72, f32[2,8,577]{2,1,0:T(8,128)S(1)} %copy-done.24, f32[2,8,577,577]{2,3,1,0:T(8,128)} %get-tuple-element.95, bf16[2,577,8,64]{1,3,2,0:T(8,128)(2,1)} %copy.125, bf16[2,577,8,64]{1,3,2,0:T(8,128)(2,1)S(1)} %copy-done.7, f32[2,577,8,64]{1,3,2,0:T(8,128)} %copy.118, ...), kind=kOutput, calls=%fused_computation.72 | convolution fusion | flops 1412810240 | bytes 48562368 | tf_op jit(solution)/shard_map/bhqk,bqhd->bkhd/dot_general | solution.py:143
  549.7 4.0 copy.151
  553.7 4.6 reshape.223
  558.3 11.4 fusion.65
  569.7 3.3 copy.152
  575.7 9.7 fusion.27
  586.3 10.1 fusion.71
  596.4 5.7 convolution_bitcast_fusion
  602.2 4.5 reduce-scatter.9.cloned.1.call-done
  606.7 107.5 %reduce-scatter.11.cloned.1.call-done = f32[128,1024]{1,0:T(8,128)} async-done(((f32[2048,1024]{1,0:T(8,128)}), f32[128,1024]{1,0:T(8,128)}) %reduce-scatter.11.cloned.1.call-update) | async-done | bytes 524304 | tf_op jit(solution)/shard_map/reduce_scatter | solution.py:186
  714.3 89.0 %reduce-scatter.5.cloned.1.call-done = f32[64,3,512]{2,0,1:T(8,128)} async-done(((f32[1024,3,512]{2,0,1:T(8,128)}), f32[64,3,512]{2,0,1:T(8,128)}) %reduce-scatter.5.cloned.1.call-update) | async-done | bytes 393232 | tf_op jit(solution)/shard_map/reduce_scatter | solution.py:183
  805.8 3.1 fusion.35
  808.9 5.1 reshape.211
  814.2 59.3 %all-reduce.1 = (f32[2,512]{1,0:T(2,128)}, f32[2048]{0:T(1024)}) all-reduce(f32[2,512]{1,0:T(2,128)S(1)} %pad_maximum_fusion, f32[2048]{0:T(1024)S(1)} %copy-done.30), channel_id=1, replica_groups=mesh['dp'=16,'tensor'=2] {'dp'}, use_global_device_ids=true, to_apply=%region_18.0 | all-reduce | flops 3072 | bytes 24576 | tf_op jit(solution)/shard_map/psum | solution.py:163
  875.4 194.0 %all-reduce.8.cloned.1.call-done = (f32[1154,1024]{1,0:T(8,128)}, f32[1154,1024]{1,0:T(8,128)}) async-done(((f32[1154,1024]{1,0:T(8,128)}, f32[1154,1024]{1,0:T(8,128)}), (f32[1154,1024]{1,0:T(8,128)}, f32[1154,1024]{1,0:T(8,128)})) %all-reduce.8.cloned.1.call-update) | async-done | bytes 9453584 | tf_op jit(solution)/shard_map/psum | solution.py:91
  1069.5 6.4 multiply_reduce_fusion.2
  1077.2 4.4 add_convert_fusion
  1083.8 3.8 copy.140
  1087.6 5.0 add_convert_fusion.1
  1094.8 3.8 copy.139
  1098.6 43.5 %all-reduce = (f32[1024]{0:T(1024)}, f32[1024]{0:T(1024)}, f32[1024]{0:T(1024)}, f32[1024]{0:T(1024)}, f32[1024]{0:T(1024)}, /*index=5*/f32[1024]{0:T(1024)}) all-reduce(f32[1024]{0:T(1024)S(1)} %dynamic-slice_reduce_fusion, f32[1024]{0:T(1024)S(1)} %get-tuple-element.72, ...), channel_id=1, replica_groups=mesh['dp'=16,'tensor'=2] {'dp','tensor'}, use_global_device_ids=true, to_apply=%region_21.0 | all-reduce | flops 6144 | bytes 49152 | tf_op jit(solution)/shard_map/psum | solution.py:171
  1142.1 4.8 all-gather.12.cloned.1.call-done
  1146.9 75.1 %all-gather.14.cloned.1.call-done = f32[2048,1024]{1,0:T(8,128)} async-done(((f32[128,1024]{1,0:T(8,128)}), f32[2048,1024]{1,0:T(8,128)}) %all-gather.14.cloned.1.call-update) | async-done | bytes 8388624 | tf_op jit(solution)/shard_map/all_gather | solution.py:192
  1222.0 62.3 %all-gather.8.cloned.1.call-done = f32[1024,3,512]{2,0,1:T(8,128)} async-done(((f32[64,3,512]{2,0,1:T(8,128)}), f32[1024,3,512]{2,0,1:T(8,128)}) %all-gather.8.cloned.1.call-update) | async-done | bytes 6291472 | tf_op jit(solution)/shard_map/all_gather | solution.py:189
  1284.3 6.9 copy.171
  1292.8 4.3 copy.173
  1298.6 3.4 copy.174
  (152 shorter events, 44.1 us)
Async XLA Ops:
  7.2 107.1 %copy-start = (bf16[512,1024]{1,0:T(8,128)(2,1)S(1)}, bf16[512,1024]{1,0:T(8,128)(2,1)}, u32[]{:S(2)}) copy-start(bf16[512,1024]{1,0:T(8,128)(2,1)} %param.19) | copy-start | bytes 3145732
  7.2 3.8 copy-start.4
  7.2 7.9 copy-start.27
  7.2 7.9 copy-start.34
  7.2 234.8 %all-reduce.6.cloned.1.call-start = ((), (), s32[]{:S(2)}) async-start(), calls=%async_computation.4 | async-start | bytes 9502720 | tf_op jit(solution)/shard_map/psum | solution.py:85
  11.0 3.3 copy-start.15
  14.4 0.7 copy-start.18
  50.1 8.3 copy-start.33
  58.5 14.0 %copy-start.25 = (f32[8,64]{1,0:T(8,128)}, f32[8,64]{1,0:T(8,128)S(1)}, u32[]{:S(2)}) copy-start(f32[8,64]{1,0:T(8,128)S(1)} %add.148) | copy-start | bytes 6148
  83.0 11.6 copy-start.23
  94.6 12.8 copy-start.6
  119.2 295.9 %all-gather.16.cloned.1.call-start = ((), (), s32[]{:S(2)}) async-start(), calls=%async_computation.13 | async-start | bytes 14254080 | tf_op jit(solution)/shard_map/all_gather | solution.py:117
  127.3 114.8 %copy-start.31 = (f32[1024]{0:T(1024)S(1)}, f32[1024]{0:T(1024)}, u32[]{:S(2)}) copy-start(f32[1024]{0:T(1024)} %param.20) | copy-start | bytes 12292
  246.4 32.0 %copy-start.1 = (f32[1154,1024]{1,0:T(8,128)}, f32[1154,1024]{1,0:T(8,128)S(1)}, u32[]{:S(2)}) copy-start(f32[1154,1024]{1,0:T(8,128)S(1)} %get-tuple-element.91) | copy-start | bytes 14180356
  246.5 0.7 copy-start.29
  246.5 3.9 copy-start.35
  246.5 3.9 copy-start.37
  246.5 3.9 copy-start.38
  250.4 28.1 %copy-start.9 = (bf16[1154,1024]{1,0:T(8,128)(2,1)S(1)}, bf16[1154,1024]{1,0:T(8,128)(2,1)}, u32[]{:S(2)}) copy-start(bf16[1154,1024]{1,0:T(8,128)(2,1)} %reshape.208) | copy-start | bytes 7090180
  250.4 28.1 %copy-start.36 = (bf16[2048,1024]{1,0:T(8,128)(2,1)S(1)}, bf16[2048,1024]{1,0:T(8,128)(2,1)}, u32[]{:S(2)}) copy-start(bf16[2048,1024]{1,0:T(8,128)(2,1)} %param.25) | copy-start | bytes 12582916
  289.4 6.8 copy-start.39
  296.2 289.3 %reduce-scatter.7.cloned.1.call-start = ((), (), s32[]{:S(2)}) async-start(), calls=%async_computation.7 | async-start | bytes 2228224 | tf_op jit(solution)/shard_map/reduce_scatter | solution.py:184
  415.1 14.0 %slice-start = ((s8[4751360]{0:T(1024)(128)(4,1)}), s8[557056]{0:T(1024)(128)(4,1)S(1)}, s32[]{:S(2)}) async-start(s8[4751360]{0:T(1024)(128)(4,1)} %bitcast.65), calls=%async_computation.15 | async-start | bytes 1114112
  422.5 6.6 slice-start.1
  422.5 7.8 copy-start.3
  422.5 8.4 copy-start.10
  430.9 4.0 copy-start.14
  432.8 2.1 copy-start.2
  437.8 168.9 %reduce-scatter.9.cloned.1.call-start = ((), (), s32[]{:S(2)}) async-start(), calls=%async_computation.9 | async-start | bytes 8912896 | tf_op jit(solution)/shard_map/reduce_scatter | solution.py:185
  449.3 1.7 copy-start.11
  449.3 265.0 %reduce-scatter.11.cloned.1.call-start = ((), (), s32[]{:S(2)}) async-start(), calls=%async_computation.11 | async-start | bytes 8912896 | tf_op jit(solution)/shard_map/reduce_scatter | solution.py:186
  461.5 341.9 %reduce-scatter.5.cloned.1.call-start = ((), (), s32[]{:S(2)}) async-start(), calls=%async_computation.5 | async-start | bytes 6684672 | tf_op jit(solution)/shard_map/reduce_scatter | solution.py:183
  465.3 6.9 copy-start.7
  472.2 13.3 %copy-start.24 = (f32[2,8,577]{2,1,0:T(8,128)S(1)}, f32[2,8,577]{2,1,0:T(8,128)}, u32[]{:S(2)}) copy-start(f32[2,8,577]{2,1,0:T(8,128)} %copy-done.23) | copy-start | bytes 110788
  512.4 8.5 copy-start.26
  549.7 8.7 copy-start.8
  585.5 290.0 %all-gather.10.cloned.1.call-start = ((), (), s32[]{:S(2)}) async-start(), calls=%async_computation.8 | async-start | bytes 2228224 | tf_op jit(solution)/shard_map/all_gather | solution.py:190
  586.2 10.2 copy-start.20
  586.2 10.2 copy-start.21
  586.2 483.2 %all-reduce.8.cloned.1.call-start = ((), (), s32[]{:S(2)}) async-start(), calls=%async_computation.14 | async-start | bytes 19005440 | tf_op jit(solution)/shard_map/psum | solution.py:91
  586.3 10.1 copy-start.17
  586.3 10.1 copy-start.22
  602.1 203.7 %copy-start.12 = (bf16[2,577,1024]{2,0,1:T(2,128)(2,1)S(1)}, bf16[2,577,1024]{2,0,1:T(2,128)(2,1)}, u32[]{:S(2)}) copy-start(bf16[2,577,1024]{2,0,1:T(2,128)(2,1)} %param.27) | copy-start | bytes 7090180
  602.1 544.8 %all-gather.12.cloned.1.call-start = ((), (), s32[]{:S(2)}) async-start(), calls=%async_computation.10 | async-start | bytes 8912896 | tf_op jit(solution)/shard_map/all_gather | solution.py:191
  606.7 615.3 %all-gather.14.cloned.1.call-start = ((), (), s32[]{:S(2)}) async-start(), calls=%async_computation.12 | async-start | bytes 8912896 | tf_op jit(solution)/shard_map/all_gather | solution.py:192
  714.3 570.0 %all-gather.8.cloned.1.call-start = ((), (), s32[]{:S(2)}) async-start(), calls=%async_computation.6 | async-start | bytes 6684672 | tf_op jit(solution)/shard_map/all_gather | solution.py:189
  808.9 5.3 copy-start.30
  808.9 260.6 %copy-start.28 = (f32[1024]{0:T(1024)S(1)}, f32[1024]{0:T(1024)}, u32[]{:S(2)}) copy-start(f32[1024]{0:T(1024)} %param.15) | copy-start | bytes 12292
  808.9 267.0 %slice-start.2 = ((s8[4751360]{0:T(1024)(128)(4,1)}), s8[557056]{0:T(1024)(128)(4,1)S(1)}, s32[]{:S(2)}) async-start(s8[4751360]{0:T(1024)(128)(4,1)} %bitcast.67), calls=%async_computation.17 | async-start | bytes 1114112
  1069.5 6.5 slice-start.3
  1069.5 7.8 copy-start.5
  1081.6 6.0 copy-start.32
  1083.7 3.9 copy-start.16
  1284.3 6.9 copy-start.19
  1284.3 8.6 copy-start.13
  1291.1 5.9 slice-start.4
  1292.8 5.8 slice-start.5
Sparse Core Ops, SparseCore 0:
  119.3 122.6 all-reduce.5
  296.3 118.6 all-gather.15
  437.9 61.7 reduce-scatter.6
  504.2 102.3 reduce-scatter.8
  611.1 103.0 reduce-scatter.10
  718.6 84.6 reduce-scatter.4
  805.5 40.7 all-gather.9
  848.8 220.6 all-reduce.7
  1071.6 75.2 all-gather.11
  1148.9 73.0 all-gather.13
  1224.2 60.0 all-gather.7
